TPU v7x, 32 devices: a whole 2x2x4 slice. The times are simulated.
32 devices in a mesh: gz: 4 (over y, x), gx: 8 (over z, core).
Axes of the slice: x: 2, y: 2, z: 4, core: 2. Of those that a mesh axis runs over, the one named last changes fastest.
Arguments:
- substrate: float32 [64, 256, 1024], P('gz', 'gx'), may hold values from 0 to 1
- catalyst: float32 [64, 256, 1024], P('gz', 'gx'), may hold values from 0 to 1
- extinction: float32 [2], replicated, may hold values from 0.25 to 1
- emission: float32 [3, 2], replicated, may hold values from 0.5 to 2
Outputs:
- substrate_next: float32 [64, 256, 1024], P('gz', 'gx')
- catalyst_next: float32 [64, 256, 1024], P('gz', 'gx')
- image: float32 [4, 256, 1024], P(None, 'gx', 'gz')
All inputs are finite; a program needn't handle non-finite values.
Results may differ from a plain program's by a relative error of at most 0.00004.
Values sent between devices are 32-bit elements; how exact they have to be, the bound alone decides.
No kernel may reach another device: no remote copies, remote signals or barrier semaphores. Data moves between devices by JAX's collectives and lax.ppermute only.
A program may use at most 64 MiB of HBM per device.

v0:
```python
import functools

import jax
import jax.numpy as jnp
from jax import lax
from jax.experimental import pallas as pl
from jax.experimental.pallas import tpu as pltpu
from jax.sharding import PartitionSpec as P


RATES = (0.16, 0.08)
FEED = 0.037
KILL = 0.06
OPTICAL = 4.0
ROWS, LANES = 8, 128

HBM = pl.BlockSpec(memory_space=pltpu.HBM)
VMEM = pl.BlockSpec(memory_space=pltpu.VMEM)
SMEM = pl.BlockSpec(memory_space=pltpu.SMEM)


def f32(*shape):
    return jax.ShapeDtypeStruct(shape, jnp.float32)


def hbm(x):
    return pltpu.with_memory_space_constraint(x, pltpu.HBM)


def lanes(x):
    return pltpu.roll(x, 1, axis=x.ndim - 1) + pltpu.roll(x, x.shape[-1] - 1, axis=x.ndim - 1)


def react(sub, cat, around_sub, around_cat):
    growth = sub * cat * cat
    sub_new = (1.0 - 6.0 * RATES[0] - FEED) * sub + RATES[0] * around_sub - growth + FEED
    cat_new = (1.0 - 6.0 * RATES[1] - FEED - KILL) * cat + RATES[1] * around_cat + growth
    return sub_new, cat_new


def plane_step(load, tiles, low_rows, high_rows, across, store, only=None):
    for tile in range(tiles) if only is None else only:
        sums, olds = [], []
        for s in range(2):
            old = load(s, tile)
            index = lax.broadcasted_iota(jnp.int32, old.shape, 0)
            above = load(s, tile - 1)[ROWS - 1 :] if tile else low_rows and low_rows[s]
            below = load(s, tile + 1)[:1] if tile < tiles - 1 else high_rows and high_rows[s]
            above = 0.0 if above is None else jnp.broadcast_to(above, old.shape)
            below = 0.0 if below is None else jnp.broadcast_to(below, old.shape)
            up = jnp.where(index == 0, above, pltpu.roll(old, 1, axis=0))
            down = jnp.where(index == ROWS - 1, below, pltpu.roll(old, ROWS - 1, axis=0))
            sums.append(lanes(old) + (up + down) + across(s, tile))
            olds.append(old)
        store(tile, *react(olds[0], olds[1], sums[0], sums[1]))


def span(tile):
    return pl.ds(tile * ROWS, ROWS)


def across_columns(tile, columns):
    return tile[:, :columns] if columns <= LANES else jnp.concatenate([tile] * (columns // LANES), axis=1)


def tile_of(inner, outer, tile, tiles):
    if 0 < tile < tiles - 1:
        return inner, span(tile - 1)
    return outer, span(1 if tile else 0)


def planes_kernel(sub, cat, up, down, sems):
    depth = sub.shape[0]
    copies = []
    for out, plane in ((up, depth - 1), (down, 0)):
        for s, field in enumerate((sub, cat)):
            copies.append(pltpu.make_async_copy(field.at[plane], out.at[s], sems.at[len(copies)]))
    for copy in copies:
        copy.start()
    for copy in copies:
        copy.wait()


def prepare_kernel(sub, cat, low, high, q_up, q_down, r_up, r_down):
    depth, rows, _ = sub.shape
    tiles = rows // ROWS
    fields = (sub, cat)
    for s, field in enumerate(fields):
        for plane in range(depth):
            for row in range(2):
                low[s, row, plane : plane + 1] = field[plane, row : row + 1]
                high[s, row, plane : plane + 1] = field[plane, rows - 2 + row : rows - 1 + row]
    for outer, inner, q, r in ((depth - 1, depth - 2, q_up, r_up), (0, 1, q_down, r_down)):

        def store(tile, sub_new, cat_new, q=q, r=r):
            out, at = tile_of(q, r, tile, tiles)
            out[0, at, :] = sub_new
            out[1, at, :] = cat_new

        plane_step(
            lambda s, tile, outer=outer: fields[s][outer, span(tile), :],
            rows // ROWS,
            None,
            None,
            lambda s, tile, inner=inner: fields[s][inner, span(tile), :],
            store,
        )


def composite(sub, cat, scale_sub, scale_cat, clear):
    keep = jnp.exp(-(scale_sub * sub + scale_cat * cat))
    weight = clear * (1.0 - keep)
    return weight * sub, weight * cat, clear * keep


def first_kernel(share, scale_hbm, emission_hbm, sub, cat, mid, values, scale, emission, sems):
    depth, rows, _ = sub.shape
    old = (sub, cat)
    copies = [
        pltpu.make_async_copy(scale_hbm, scale, sems.at[0]),
        pltpu.make_async_copy(emission_hbm, emission, sems.at[1]),
    ]
    for copy in copies:
        copy.start()

    @pl.loop(1, depth - 1)
    def _(k):
        def store(tile, sub_new, cat_new):
            mid[0, k, span(tile), :] = sub_new
            mid[1, k, span(tile), :] = cat_new

        plane_step(
            lambda s, tile: old[s][k, span(tile), :],
            rows // ROWS,
            None,
            None,
            lambda s, tile: old[s][k - 1, span(tile), :] + old[s][k + 1, span(tile), :],
            store,
        )

    for copy in copies:
        copy.wait()
    shape = values.shape[1:]
    for s in range(2):
        values[s] = jnp.full(shape, scale[s] * share, jnp.float32)
        for channel in range(3):
            values[2 + channel * 2 + s] = jnp.full(shape, emission[s, channel], jnp.float32)


def image_step(k, load, tiles, only, low_rows, high_rows, scales, seen, keep):
    def store(tile, sub, cat):
        at = span(tile)
        keep(tile, sub, cat)
        one, two, clear = composite(sub, cat, *scales, seen[2, at, :])
        seen[0, at, :] += one
        seen[1, at, :] += two
        seen[2, at, :] = clear

    plane_step(
        lambda s, tile: load(s, k, tile),
        tiles,
        low_rows,
        high_rows,
        lambda s, tile: load(s, k - 1, tile) + load(s, k + 1, tile),
        store,
        only,
    )


def clear_image(seen):
    seen[0] = jnp.zeros(seen.shape[1:], jnp.float32)
    seen[1] = jnp.zeros(seen.shape[1:], jnp.float32)
    seen[2] = jnp.ones(seen.shape[1:], jnp.float32)


def center_kernel(values, mid, new, seen):
    depth, rows, columns = mid.shape[1:]
    tiles = rows // ROWS
    scales = across_columns(values[0], columns), across_columns(values[1], columns)
    clear_image(seen)

    @pl.loop(2, depth - 2)
    def _(k):
        def keep(tile, sub, cat):
            new[0, k, span(tile - 1), :] = sub
            new[1, k, span(tile - 1), :] = cat

        image_step(
            k, lambda s, k, tile: mid[s, k, span(tile), :], tiles, range(1, tiles - 1), None, None, scales, seen, keep
        )


def second_kernel(
    values, mid, q_up, q_down, r_up, r_down, from_low, from_high, own_low, own_high, center, done,
    sub_out, cat_out, new, seen, near, far, rows_low, rows_high,
    heads, tails, sems,
):
    depth, rows, columns = sub_out.shape
    tiles = rows // ROWS
    scales = across_columns(values[0], columns), across_columns(values[1], columns)
    planes = pl.ds(2, depth - 4)
    copies = [
        pltpu.make_async_copy(done.at[s, planes], out.at[planes, pl.ds(ROWS, rows - 2 * ROWS)], sems.at[s])
        for s, out in enumerate((sub_out, cat_out))
    ]
    for copy in copies:
        copy.start()

    which = lax.broadcasted_iota(jnp.int32, (depth, columns), 0)
    for got, at, own, at_own, out in (
        (from_low, 1, own_low, 0, rows_low),
        (from_high, 0, own_high, 1, rows_high),
    ):
        sums, olds = [], []
        for s in range(2):
            here = got[s, at]
            ahead = jnp.where(which == 0, 0.0, pltpu.roll(here, 1, axis=0))
            behind = jnp.where(which == depth - 1, 0.0, pltpu.roll(here, depth - 1, axis=0))
            sums.append(lanes(here) + (got[s, 1 - at] + own[s, at_own]) + (ahead + behind))
            olds.append(here)
        sub, cat = react(olds[0], olds[1], sums[0], sums[1])
        out[0] = sub
        out[1] = cat

    index = lax.broadcasted_iota(jnp.int32, (ROWS, columns), 0)

    def with_low(s, k, tile):
        row = jnp.broadcast_to(from_low[s, 1, pl.ds(k, 1)], tile.shape)
        return tile + jnp.where(index == 0, RATES[s] * row, 0.0)

    def with_high(s, k, tile):
        row = jnp.broadcast_to(from_high[s, 0, pl.ds(k, 1)], tile.shape)
        return tile + jnp.where(index == ROWS - 1, RATES[s] * row, 0.0)

    @pl.loop(1, depth - 1)
    def _(k):
        for s in range(2):
            heads[s, k] = with_low(s, k, mid[s, k, span(0), :])
            tails[s, k] = with_high(s, k, mid[s, k, span(tiles - 1), :])

    def load(s, k, tile):
        if tile == 0:
            return heads[s, k]
        if tile == tiles - 1:
            return tails[s, k]
        return mid[s, k, span(tile), :]

    for s in range(2):
        for tile in range(tiles):
            down, at = tile_of(q_down, r_down, tile, tiles)
            up, at = tile_of(q_up, r_up, tile, tiles)
            first, last = down[s, at, :], up[s, at, :]
            if tile == 0:
                first, last = with_low(s, 0, first), with_low(s, depth - 1, last)
            if tile == tiles - 1:
                first, last = with_high(s, 0, first), with_high(s, depth - 1, last)
            near[s, 0, span(tile), :] = first
            far[s, 2, span(tile), :] = last
            for j in range(2):
                near[s, 1 + j, span(tile), :] = load(s, 1 + j, tile)
                far[s, j, span(tile), :] = load(s, depth - 3 + j, tile)

    clear_image(seen)
    for tile in range(1, tiles - 1):
        for part in range(3):
            seen[part, span(tile), :] = center[part, span(tile), :]

    @pl.loop(2, depth - 2)
    def _(k):
        def keep(tile, sub, cat):
            new[0, 1 if tile else 0, k] = sub
            new[1, 1 if tile else 0, k] = cat

        image_step(
            k,
            load,
            tiles,
            (0, tiles - 1),
            [rows_low[s, pl.ds(k, 1)] for s in range(2)],
            [rows_high[s, pl.ds(k, 1)] for s in range(2)],
            scales,
            seen,
            keep,
        )

    for copy in copies:
        copy.wait()


def rows_kernel(r_up, r_down, from_low, from_high, up, down):
    depth = from_low.shape[2]
    for plane, r, out in ((depth - 1, r_up, up), (0, r_down, down)):
        for place, edge, source in ((0, 0, from_low.at[:, 1]), (1, ROWS - 1, from_high.at[:, 0])):
            for s in range(2):
                tile = r[s, span(place), :]
                index = lax.broadcasted_iota(jnp.int32, tile.shape, 0)
                row = jnp.broadcast_to((2.0 * RATES[s]) * source[s, plane : plane + 1], tile.shape)
                out[s, span(place), :] = tile + jnp.where(index == edge, row, 0.0)


def rim_kernel(
    values, p_low, p_high, down, up, near, far, rows_low, rows_high, inner,
    ring, known, seen, mid,
):
    depth = rows_low.shape[1]
    rows, columns = inner.shape[1:]
    tiles = rows // ROWS
    scale_sub, scale_cat = across_columns(values[0], columns), across_columns(values[1], columns)
    for side, p, own, inside in ((0, p_low, down, near), (1, p_high, up, far)):
        zero, one, two = (0, 1, 2) if side == 0 else (2, 1, 0)
        outer, beside = (0, 1) if side == 0 else (depth - 1, depth - 2)
        for s in range(2):
            mid[side, s] = inside[s, zero] + RATES[s] * p[s]

        def store_known(tile, sub, cat, side=side, own=own):
            at = span(tile)
            known[side, 0, at, :] = sub + (RATES[0] * RATES[0]) * own[0, at, :]
            known[side, 1, at, :] = cat + (RATES[1] * RATES[1]) * own[1, at, :]

        plane_step(
            lambda s, tile, side=side: mid[side, s, span(tile), :],
            tiles,
            [rows_low[s, outer : outer + 1] for s in range(2)],
            [rows_high[s, outer : outer + 1] for s in range(2)],
            lambda s, tile, inside=inside, one=one: inside[s, one, span(tile), :],
            store_known,
        )

        def store_ring(tile, sub, cat, side=side):
            ring[0, side, span(tile), :] = sub
            ring[1, side, span(tile), :] = cat

        plane_step(
            lambda s, tile, inside=inside, one=one: inside[s, one, span(tile), :],
            tiles,
            [rows_low[s, beside : beside + 1] for s in range(2)],
            [rows_high[s, beside : beside + 1] for s in range(2)],
            lambda s, tile, inside=inside, two=two, side=side: inside[s, two, span(tile), :]
            + mid[side, s, span(tile), :],
            store_ring,
        )

    for tile in range(tiles):
        at = span(tile)
        one, two, clear = composite(ring[0, 0, at, :], ring[1, 0, at, :], scale_sub, scale_cat, 1.0)
        sub = one + clear * inner[0, at, :]
        cat = two + clear * inner[1, at, :]
        clear = clear * inner[2, at, :]
        one, two, clear = composite(ring[0, 1, at, :], ring[1, 1, at, :], scale_sub, scale_cat, clear)
        seen[0, at, :] = sub + one
        seen[1, at, :] = cat + two
        seen[2, at, :] = clear


def partner(index, shift, count):
    return index ^ shift if count & (count - 1) == 0 else (index + shift) % count


def origin(index, shift, count):
    return index ^ shift if count & (count - 1) == 0 else (index + count - shift) % count


def finish(values, known, seen, low, high, tiles, outer, whole, where):
    columns = seen.shape[2]
    scales = across_columns(values[0], columns), across_columns(values[1], columns)
    for place, tile in enumerate(tiles):
        at, to = span(tile), span(place)
        planes = []
        for side, q in enumerate((low, high)):
            for s in range(2):
                value = known[side, s, at, :] + RATES[s] * q[s, to, :]
                outer[s, side, to, :] = value
                planes.append(value)
        one, two, clear = composite(planes[0], planes[1], *scales, 1.0)
        sub = one + clear * seen[0, at, :]
        cat = two + clear * seen[1, at, :]
        clear = clear * seen[2, at, :]
        one, two, clear = composite(planes[2], planes[3], *scales, clear)
        whole[0, where(tile), :] = sub + one
        whole[1, where(tile), :] = cat + two
        whole[2, where(tile), :] = clear


def cut(whole, rows, piece, to, target, count):
    wide = whole.shape[2] // count
    if wide % LANES == 0:
        piece[:, to, :] = whole[:, rows, pl.ds(pl.multiple_of(target * wide, LANES), wide)]
        return
    for other in range(count):

        @pl.when(target == other)
        def _(other=other):
            piece[:, to, :] = whole[:, rows, other * wide : (other + 1) * wide]


def most_kernel(count, values, known, q_low, q_high, seen, piece, outer, whole):
    tiles = seen.shape[1] // ROWS
    finish(values, known, seen, q_low, q_high, range(1, tiles - 1), outer, whole, lambda tile: span(tile - 1))
    everything = pl.ds(0, piece.shape[1])
    cut(whole, everything, piece, everything, partner(lax.axis_index("gz"), count // 2, count), count)


def last_kernel(values, known, r_low, r_high, seen, most, *rest):
    *pieces, outer, whole = rest
    rows = seen.shape[1]
    tiles = rows // ROWS
    count = len(pieces)
    finish(values, known, seen, r_low, r_high, (0, tiles - 1), outer, whole, span)
    inside = pl.ds(ROWS, rows - 2 * ROWS)
    whole[:, inside, :] = most[...]
    me = lax.axis_index("gz")
    for shift, piece in enumerate(pieces):
        target = partner(me, shift, count)
        if piece.shape[1] == rows:
            everything = pl.ds(0, rows)
            cut(whole, everything, piece, everything, target, count)
        else:
            cut(whole, pl.ds(0, ROWS), piece, span(0), target, count)
            cut(whole, pl.ds(rows - ROWS, ROWS), piece, span(1), target, count)


def lanes_of(block, wide):
    return pl.ds(pl.multiple_of(block * wide, LANES), wide)


def foreign_kernel(count, q_up, q_down, up, down):
    wide = q_up.shape[2] // count
    me = lax.axis_index("gz")
    for q, out, target in ((q_up, up, (me + 1) % count), (q_down, down, (me + count - 1) % count)):
        for block in range(count - 1):
            out[:, :, block * wide : (block + 1) * wide] = q[:, :, lanes_of((target + 1 + block) % count, wide)]


def split_kernel(count, m_up, m_down, q_up, q_down, up, down, own_up, own_down):
    outers = m_up.shape[1]
    wide = m_up.shape[2] // count
    rows = own_up.shape[1]
    me = lax.axis_index("gz")
    for m, q, out, own, target in (
        (m_up, q_up, up, own_up, (me + 1) % count),
        (m_down, q_down, down, own_down, (me + count - 1) % count),
    ):
        for block in range(count - 1):
            out[:, :, block * wide : (block + 1) * wide] = m[:, :, lanes_of((target + 1 + block) % count, wide)]
        mine = lanes_of(target, wide)
        own[:, :ROWS, :] = m[:, :ROWS, mine]
        own[:, pl.ds(ROWS, rows - outers), :] = q[:, :, mine]
        own[:, rows - ROWS :, :] = m[:, ROWS:, mine]


def finish_tile(scales, low, high, seen):
    one, two, clear = composite(low[0], low[1], *scales, 1.0)
    sub = one + clear * seen[0]
    cat = two + clear * seen[1]
    clear = clear * seen[2]
    one, two, clear = composite(high[0], high[1], *scales, clear)
    return sub + one, cat + two, clear


def others_kernel(values, known, q_low, q_high, r_low, r_high, seen, *pieces_and_outer):
    *pieces, outer = pieces_and_outer
    rows, columns = seen.shape[1:]
    count = len(pieces) + 1
    wide = columns // count
    tiles = rows // ROWS
    scales = across_columns(values[0], wide), across_columns(values[1], wide)
    me = lax.axis_index("gz")
    for shift, piece in enumerate(pieces, 1):
        owner = partner(me, shift, count)
        there = lanes_of(owner, wide)
        sent = lanes_of((owner + count - me - 1) % count, wide)
        for tile in range(tiles):
            at = span(tile)
            ends = []
            for side, (q, r) in enumerate(((q_low, r_low), (q_high, r_high))):
                got, place = tile_of(q, r, tile, tiles)
                ends.append([known[side, s, at, there] + RATES[s] * got[s, place, sent] for s in range(2)])
                for s in range(2):
                    outer[s, side, at, there] = ends[side][s]
            result = finish_tile(scales, ends[0], ends[1], [seen[part, at, there] for part in range(3)])
            for part in range(3):
                piece[part, at, :] = result[part]


def own_kernel(values, known, o_low, o_high, seen, piece, outer):
    rows, wide = piece.shape[1:]
    scales = across_columns(values[0], wide), across_columns(values[1], wide)
    here = lanes_of(lax.axis_index("gz"), wide)
    for tile in range(rows // ROWS):
        at = span(tile)
        ends = []
        for side, o in enumerate((o_low, o_high)):
            ends.append([known[side, s, at, here] + RATES[s] * o[s, at, :] for s in range(2)])
            for s in range(2):
                outer[s, side, at, :] = ends[side][s]
        result = finish_tile(scales, ends[0], ends[1], [seen[part, at, here] for part in range(3)])
        for part in range(3):
            piece[part, at, :] = result[part]


def put_kernel(count, new, ring, others, own, sub_in, cat_in, sub_out, cat_out, sems):
    del sub_in, cat_in
    depth, rows, columns = sub_out.shape
    wide = columns // count
    planes = pl.ds(2, depth - 4)
    me = lax.axis_index("gz")
    copies = []
    for s, out in enumerate((sub_out, cat_out)):
        targets = []
        for end in range(2):
            targets.append((new.at[s, end, planes], out.at[planes, pl.ds(end * (rows - ROWS), ROWS)]))
        for side in range(2):
            plane = side * (depth - 1)
            targets.append((ring.at[s, side], out.at[1 + side * (depth - 3)]))
            targets.append((own.at[s, side], out.at[plane, :, lanes_of(me, wide)]))
            for shift in range(1, count):
                there = lanes_of(partner(me, shift, count), wide)
                targets.append((others.at[s, side, :, there], out.at[plane, :, there]))
        for source, target in targets:
            copies.append(pltpu.make_async_copy(source, target, sems.at[len(copies)]))
    for copy in copies:
        copy.start()
    for copy in copies:
        copy.wait()


def paint_kernel(values, *pieces_and_rest):
    *pieces, image, slabs = pieces_and_rest
    count = len(pieces)
    me = lax.axis_index("gz")
    for shift, piece in enumerate(pieces):
        slabs[origin(me, shift, count)] = piece[...]
    shade(values, slabs, image, count)


def shade(values, slabs, image, count):
    rows, wide = image.shape[1:]
    for tile in range(rows // ROWS):
        at = span(tile)
        sub, cat, clear = slabs[0, 0, at, :], slabs[0, 1, at, :], slabs[0, 2, at, :]
        for slab in range(1, count):
            sub = sub + clear * slabs[slab, 0, at, :]
            cat = cat + clear * slabs[slab, 1, at, :]
            clear = clear * slabs[slab, 2, at, :]
        for channel in range(3):
            of_sub = across_columns(values[2 + channel * 2], wide)
            of_cat = across_columns(values[3 + channel * 2], wide)
            image[channel, at, :] = of_sub * sub + of_cat * cat
        image[3, at, :] = 1.0 - clear


def shade_kernel(values, half, *pieces_and_rest):
    *pieces, image, slabs = pieces_and_rest
    count = len(pieces)
    rows, _ = image.shape[1:]
    me = lax.axis_index("gz")
    for shift, piece in enumerate(pieces):
        slab = origin(me, shift, count)
        if piece.shape[1] == rows:
            slabs[slab] = piece[...]
        else:
            slabs[slab, :, pl.ds(ROWS, rows - 2 * ROWS), :] = half[...]
            slabs[slab, :, span(0), :] = piece[:, :ROWS]
            slabs[slab, :, pl.ds(rows - ROWS, ROWS), :] = piece[:, ROWS:]
    shade(values, slabs, image, count)


def place_kernel(new, ring, inner, outer, sub_in, cat_in, sub_out, cat_out, sems):
    del sub_in, cat_in
    depth, rows, _ = sub_out.shape
    planes = pl.ds(2, depth - 4)
    copies = []
    for s, out in enumerate((sub_out, cat_out)):
        for end in range(2):
            target = out.at[planes, pl.ds(end * (rows - ROWS), ROWS)]
            copies.append(pltpu.make_async_copy(new.at[s, end, planes], target, sems.at[len(copies)]))
        for side in range(2):
            plane = side * (depth - 1)
            for source, target in (
                (ring.at[s, side], out.at[1 + side * (depth - 3)]),
                (inner.at[s, side], out.at[plane, pl.ds(ROWS, rows - 2 * ROWS)]),
                (outer.at[s, side, span(0)], out.at[plane, span(0)]),
                (outer.at[s, side, span(1)], out.at[plane, pl.ds(rows - ROWS, ROWS)]),
            ):
                copies.append(pltpu.make_async_copy(source, target, sems.at[len(copies)]))
    for copy in copies:
        copy.start()
    for copy in copies:
        copy.wait()


def call(kernel, flops, room, **kwargs):
    return pl.pallas_call(
        kernel,
        cost_estimate=pl.CostEstimate(flops=flops, bytes_accessed=1 << 16, transcendentals=0),
        compiler_params=pltpu.CompilerParams(vmem_limit_bytes=room << 20),
        **kwargs,
    )


def body(substrate, catalyst, extinction, emission):
    depth, rows, columns = substrate.shape
    count = lax.axis_size("gz")
    wide = columns // count
    share = OPTICAL / (depth * count)
    middle = rows - 2 * ROWS

    def ring(size, shift):
        return [(i, (i + shift) % size) for i in range(size)]

    def shifted(x, axis, shift):
        return lax.ppermute(x, axis, ring(lax.axis_size(axis), shift))

    up, down = call(
        planes_kernel,
        1 << 20,
        2,
        name="planes",
        out_shape=(f32(2, rows, columns),) * 2,
        in_specs=[HBM, HBM],
        out_specs=(VMEM,) * 2,
        scratch_shapes=[pltpu.SemaphoreType.DMA((4,))],
    )(hbm(substrate), hbm(catalyst))
    p_low = shifted(up, "gz", 1)
    p_high = shifted(down, "gz", -1)

    own_low, own_high, q_up, q_down, r_up, r_down = call(
        prepare_kernel,
        1 << 22,
        2,
        name="prepare",
        out_shape=(f32(2, 2, depth, columns),) * 2 + (f32(2, middle, columns),) * 2 + (f32(2, 2 * ROWS, columns),) * 2,
        in_specs=[VMEM] * 2,
        out_specs=(VMEM,) * 6,
    )(substrate, catalyst)
    from_low = shifted(own_high, "gx", 1)
    from_high = shifted(own_low, "gx", -1)
    split = wide % LANES == 0
    foreign = columns - wide
    if split:
        q_sent = call(
            functools.partial(foreign_kernel, count),
            1 << 18,
            2,
            name="foreign",
            out_shape=(f32(2, middle, foreign),) * 2,
            in_specs=[VMEM] * 2,
            out_specs=(VMEM,) * 2,
        )(q_up, q_down)
    else:
        q_sent = (q_up, q_down)
    q_low = shifted(q_sent[0], "gz", 1)
    q_high = shifted(q_sent[1], "gz", -1)

    mid, values = call(
        functools.partial(first_kernel, share),
        1 << 24,
        2,
        name="first",
        out_shape=(f32(2, depth, rows, columns), f32(8, ROWS, LANES)),
        in_specs=[HBM, HBM, VMEM, VMEM],
        out_specs=(VMEM, VMEM),
        scratch_shapes=[
            pltpu.SMEM((2,), jnp.float32),
            pltpu.SMEM((2, 3), jnp.float32),
            pltpu.SemaphoreType.DMA((2,)),
        ],
    )(hbm(extinction), hbm(emission.T), substrate, catalyst)
    done, center = call(
        center_kernel,
        1 << 24,
        2,
        name="center",
        out_shape=(f32(2, depth, middle, columns), f32(3, rows, columns)),
        in_specs=[VMEM, VMEM],
        out_specs=(VMEM, VMEM),
    )(values, mid)

    m_up, m_down = call(
        rows_kernel,
        1 << 18,
        2,
        name="rows",
        out_shape=(f32(2, 2 * ROWS, columns),) * 2,
        in_specs=[VMEM] * 4,
        out_specs=(VMEM,) * 2,
    )(r_up, r_down, from_low, from_high)
    if split:
        m_up, m_down, o_up, o_down = call(
            functools.partial(split_kernel, count),
            1 << 18,
            2,
            name="split",
            out_shape=(f32(2, 2 * ROWS, foreign),) * 2 + (f32(2, rows, wide),) * 2,
            in_specs=[VMEM] * 4,
            out_specs=(VMEM,) * 4,
        )(m_up, m_down, q_up, q_down)
        o_low = shifted(o_up, "gz", 1)
        o_high = shifted(o_down, "gz", -1)
    r_low = shifted(m_up, "gz", 1)
    r_high = shifted(m_down, "gz", -1)

    sub_part, cat_part, new, inner, near, far, rows_low, rows_high = call(
        second_kernel,
        1 << 25,
        4,
        name="second",
        out_shape=(
            f32(depth, rows, columns),
            f32(depth, rows, columns),
            f32(2, 2, depth, ROWS, columns),
            f32(3, rows, columns),
            f32(2, 3, rows, columns),
            f32(2, 3, rows, columns),
            f32(2, depth, columns),
            f32(2, depth, columns),
        ),
        in_specs=[VMEM] * 12,
        out_specs=(HBM, HBM) + (VMEM,) * 6,
        scratch_shapes=[
            pltpu.VMEM((2, depth, ROWS, columns), jnp.float32),
            pltpu.VMEM((2, depth, ROWS, columns), jnp.float32),
            pltpu.SemaphoreType.DMA((2,)),
        ],
    )(values, mid, q_up, q_down, r_up, r_down, from_low, from_high, own_low, own_high, center, done)

    p_low, p_high, inner = lax.optimization_barrier((p_low, p_high, inner))
    ring_planes, known, seen = call(
        rim_kernel,
        1 << 23,
        4,
        name="rim",
        out_shape=(f32(2, 2, rows, columns), f32(2, 2, rows, columns), f32(3, rows, columns)),
        in_specs=[VMEM] * 10,
        out_specs=(VMEM,) * 3,
        scratch_shapes=[pltpu.VMEM((2, 2, rows, columns), jnp.float32)],
    )(values, p_low, p_high, down, up, near, far, rows_low, rows_high, inner)

    def paired(piece, shift):
        return lax.ppermute(piece, "gz", [(i, int(partner(i, shift, count))) for i in range(count)])

    if split:
        *pieces, others = call(
            others_kernel,
            1 << 22,
            2,
            name="others",
            out_shape=(f32(3, rows, wide),) * (count - 1) + (f32(2, 2, rows, columns),),
            in_specs=[VMEM] * 7,
            out_specs=(VMEM,) * count,
        )(values, known, q_low, q_high, r_low, r_high, seen)
        received = [None] * count
        half = count // 2
        for shift in [i for i in range(count - 1, 0, -1) if i != half] + [half]:
            received[shift] = paired(pieces[shift - 1], shift)
        received[0], own = call(
            own_kernel,
            1 << 20,
            2,
            name="own",
            out_shape=(f32(3, rows, wide), f32(2, 2, rows, wide)),
            in_specs=[VMEM] * 5,
            out_specs=(VMEM,) * 2,
        )(values, known, o_low, o_high, seen)
        sub_final, cat_final = call(
            functools.partial(put_kernel, count),
            1 << 22,
            2,
            name="put",
            out_shape=(f32(depth, rows, columns), f32(depth, rows, columns)),
            in_specs=[VMEM, VMEM, VMEM, VMEM, HBM, HBM],
            out_specs=(HBM, HBM),
            input_output_aliases={4: 0, 5: 1},
            scratch_shapes=[pltpu.SemaphoreType.DMA((4 * (count + 2),))],
        )(new, ring_planes, others, own, sub_part, cat_part)
        image = call(
            paint_kernel,
            1 << 20,
            4,
            name="paint",
            out_shape=f32(4, rows, wide),
            in_specs=[VMEM] * (1 + count),
            out_specs=VMEM,
            scratch_shapes=[pltpu.VMEM((count, 3, rows, wide), jnp.float32)],
        )(values, *received)
        return sub_final, cat_final, image

    half = count // 2
    half_piece, inner_rows, most = call(
        functools.partial(most_kernel, count),
        1 << 22,
        2,
        name="most",
        out_shape=(f32(3, middle, wide), f32(2, 2, middle, columns), f32(3, middle, columns)),
        in_specs=[VMEM] * 5,
        out_specs=(VMEM,) * 3,
    )(values, known, q_low, q_high, seen)

    half_piece = paired(half_piece, half)

    *pieces, outer_rows = call(
        last_kernel,
        1 << 22,
        4,
        name="last",
        out_shape=tuple(f32(3, 2 * ROWS if shift == half else rows, wide) for shift in range(count))
        + (f32(2, 2, 2 * ROWS, columns),),
        in_specs=[VMEM] * 6,
        out_specs=(VMEM,) * (count + 1),
        scratch_shapes=[pltpu.VMEM((3, rows, columns), jnp.float32)],
    )(values, known, r_low, r_high, seen, most)

    received = [pieces[0]] * count
    for shift in range(count - 1, 0, -1):
        received[shift] = paired(pieces[shift], shift)

    sub_final, cat_final = call(
        place_kernel,
        1 << 22,
        2,
        name="place",
        out_shape=(f32(depth, rows, columns), f32(depth, rows, columns)),
        in_specs=[VMEM, VMEM, VMEM, VMEM, HBM, HBM],
        out_specs=(HBM, HBM),
        input_output_aliases={4: 0, 5: 1},
        scratch_shapes=[pltpu.SemaphoreType.DMA((20,))],
    )(new, ring_planes, inner_rows, outer_rows, sub_part, cat_part)

    image = call(
        shade_kernel,
        1 << 20,
        4,
        name="shade",
        out_shape=f32(4, rows, wide),
        in_specs=[VMEM] * (2 + count),
        out_specs=VMEM,
        scratch_shapes=[pltpu.VMEM((count, 3, rows, wide), jnp.float32)],
    )(values, half_piece, *received)
    return sub_final, cat_final, image


def solution(mesh):
    placed = (P("gz", "gx", None), P("gz", "gx", None), P(), P())

    return jax.shard_map(
        body,
        mesh=mesh,
        in_specs=placed,
        out_specs=(P("gz", "gx", None), P("gz", "gx", None), P(None, "gx", "gz")),
        check_vma=False,
    )
```

profile of v0, /device:TPU:0, one launch (start us, length us, event | category | flops | bytes accessed | tf_op | source)
XLA Modules:
  0.0 44.0 jit_solution(4250884401894096115)
XLA Ops:
  0.6 0.0 copy-start
  0.6 1.6 %copy-done = f32[16,32,1024]{2,1,0:T(8,128)S(1)} copy-done((f32[16,32,1024]{2,1,0:T(8,128)S(1)}, f32[16,32,1024]{2,1,0:T(8,128)}, u32[]{:S(2)}) %copy-start) | copy-done | bytes 2097176
  2.2 0.0 copy-start.2
  2.2 1.6 %copy-done.2 = f32[16,32,1024]{2,1,0:T(8,128)S(1)} copy-done((f32[16,32,1024]{2,1,0:T(8,128)S(1)}, f32[16,32,1024]{2,1,0:T(8,128)}, u32[]{:S(2)}) %copy-start.2) | copy-done | bytes 2097176
  3.8 0.5 %prepare.1 = (f32[2,2,16,1024]{3,2,1,0:T(8,128)S(1)}, f32[2,2,16,1024]{3,2,1,0:T(8,128)S(1)}, f32[2,16,1024]{2,1,0:T(8,128)S(1)}, f32[2,16,1024]{2,1,0:T(8,128)S...) custom-call(f32[16,32,1024]{2,1,0:T(8,128)S(1)} %copy-done, f32[16,32,1024]{2,1,0:T(8,128)S(1)} %copy-done.2), custom_call_target="tpu_custom_call" | custom-call | flops 4194304 | bytes 65536 | tf_op jit(solution)/shard_map/prepare/pallas_call | solution.py:627
  4.3 0.5 %collective-permute-start = (f32[2,2,16,1024]{3,2,1,0:T(8,128)S(1)}, f32[2,2,16,1024]{3,2,1,0:T(8,128)S(1)}, u32[]{:S(2)}, u32[]{:S(2)}) collective-permute-start(f32[2,2,16,1024]{3,2,1,0:T(8,128)S(1)} %get-tuple-element.51.own_high), channel_id=1, source_target_pairs={{0,1},{1,2},{2,3},{3,4},{4,5},{5,6},{6,7},{7,0},{8,9},{9,10},{10,1... | collective-permute-start | bytes 786440 | tf_op jit(solution)/shard_map/ppermute | solution.py:612
  4.8 0.0 copy-start.1
  4.8 0.0 copy-start.3
  4.8 4.1 %collective-permute-start.1 = (f32[2,2,16,1024]{3,2,1,0:T(8,128)S(1)}, f32[2,2,16,1024]{3,2,1,0:T(8,128)S(1)}, u32[]{:S(2)}, u32[]{:S(2)}) collective-permute-start(f32[2,2,16,1024]{3,2,1,0:T(8,128)S(1)} %get-tuple-element.52.own_low), channel_id=1, source_target_pairs={{0,7},{1,0},{2,1},{3,2},{4,3},{5,4},{6,5},{7,6},{8,15},{9,8},{10,9... | collective-permute-start | bytes 786440 | tf_op jit(solution)/shard_map/ppermute | solution.py:612
  8.9 1.1 %planes.1 = (f32[2,32,1024]{2,1,0:T(8,128)S(1)}, f32[2,32,1024]{2,1,0:T(8,128)S(1)}) custom-call(f32[16,32,1024]{2,1,0:T(8,128)} %sub.5, f32[16,32,1024]{2,1,0:T(8,128)} %cat.5), custom_call_target="tpu_custom_call" | custom-call | flops 1048576 | bytes 65536 | tf_op jit(solution)/shard_map/planes/pallas_call | solution.py:614
  10.1 2.0 %collective-permute-start.2 = (f32[2,32,1024]{2,1,0:T(8,128)S(1)}, f32[2,32,1024]{2,1,0:T(8,128)S(1)}, u32[]{:S(2)}, u32[]{:S(2)}) collective-permute-start(f32[2,32,1024]{2,1,0:T(8,128)S(1)} %get-tuple-element.56.up), channel_id=1, source_target_pairs={{0,8},{8,16},{16,24},{24,0},{1,9},{9,17},{17,25},{25,1},{2,10},{10... | collective-permute-start | bytes 786440 | tf_op jit(solution)/shard_map/ppermute | solution.py:612
  12.0 1.0 %collective-permute-start.3 = (f32[2,32,1024]{2,1,0:T(8,128)S(1)}, f32[2,32,1024]{2,1,0:T(8,128)S(1)}, u32[]{:S(2)}, u32[]{:S(2)}) collective-permute-start(f32[2,32,1024]{2,1,0:T(8,128)S(1)} %get-tuple-element.57.down), channel_id=1, source_target_pairs={{0,24},{8,0},{16,8},{24,16},{1,25},{9,1},{17,9},{25,17},{2,26},{10... | collective-permute-start | bytes 786440 | tf_op jit(solution)/shard_map/ppermute | solution.py:612
  13.1 1.1 %collective-permute-start.4 = (f32[2,16,768]{2,1,0:T(8,128)S(1)}, f32[2,16,768]{2,1,0:T(8,128)S(1)}, u32[]{:S(2)}, u32[]{:S(2)}) collective-permute-start(f32[2,16,768]{2,1,0:T(8,128)S(1)} %get-tuple-element.68), channel_id=1, source_target_pairs={{0,8},{8,16},{16,24},{24,0},{1,9},{9,17},{17,25},{25,1},{2,10},{10... | collective-permute-start | bytes 294920 | tf_op jit(solution)/shard_map/ppermute | solution.py:612
  14.1 0.0 collective-permute-done.from_low
  14.1 2.4 %collective-permute-start.5 = (f32[2,16,768]{2,1,0:T(8,128)S(1)}, f32[2,16,768]{2,1,0:T(8,128)S(1)}, u32[]{:S(2)}, u32[]{:S(2)}) collective-permute-start(f32[2,16,768]{2,1,0:T(8,128)S(1)} %get-tuple-element.69), channel_id=1, source_target_pairs={{0,24},{8,0},{16,8},{24,16},{1,25},{9,1},{17,9},{25,17},{2,26},{10... | collective-permute-start | bytes 294920 | tf_op jit(solution)/shard_map/ppermute | solution.py:612
  16.6 0.0 collective-permute-done.1.from_high
  16.7 0.1 collective-permute-start.6
  16.7 3.5 %collective-permute-done.2.p_low = f32[2,32,1024]{2,1,0:T(8,128)S(1)} collective-permute-done((f32[2,32,1024]{2,1,0:T(8,128)S(1)}, f32[2,32,1024]{2,1,0:T(8,128)S(1)}, u32[]{:S(2)}, u32[]{:S(2)}) %collective-permute-start.2) | collective-permute-done | bytes 262176 | tf_op jit(solution)/shard_map/ppermute | solution.py:612
  20.2 2.0 %collective-permute-start.7 = (f32[2,16,768]{2,1,0:T(8,128)S(1)}, f32[2,16,768]{2,1,0:T(8,128)S(1)}, u32[]{:S(2)}, u32[]{:S(2)}) collective-permute-start(f32[2,16,768]{2,1,0:T(8,128)S(1)} %get-tuple-element.73), channel_id=1, source_target_pairs={{0,24},{8,0},{16,8},{24,16},{1,25},{9,1},{17,9},{25,17},{2,26},{10... | collective-permute-start | bytes 294920 | tf_op jit(solution)/shard_map/ppermute | solution.py:612
  22.2 0.0 copy-done.1
  22.2 0.0 copy-done.3
  22.2 3.0 %first.1 = (f32[2,16,32,1024]{3,2,1,0:T(8,128)S(1)}, f32[8,8,128]{2,1,0:T(8,128)S(1)}) custom-call(f32[2]{0:T(128)} %scale_hbm.1, f32[2,3]{1,0:T(2,128)} %bitcast.1, f32[16,32,1024]{2,1,0:T(8,128)S(1)} %copy-done.1, f32[16,32,1024]{2,1,0:T(8,128)S(1)} %copy-done.3), custom_call_target="tpu_custom_call" | custom-call | flops 16777216 | bytes 65536 | tf_op jit(solution)/shard_map/first/pallas_call | solution.py:655
  25.2 2.1 %center.1 = (f32[2,16,16,1024]{3,2,1,0:T(8,128)S(1)}, f32[3,32,1024]{2,1,0:T(8,128)S(1)}) custom-call(f32[8,8,128]{2,1,0:T(8,128)S(1)} %get-tuple-element.45.values, f32[2,16,32,1024]{3,2,1,0:T(8,128)S(1)} %get-tuple-element.46.mid), custom_call_target="tpu_custom_call" | custom-call | flops 16777216 | bytes 65536 | tf_op jit(solution)/shard_map/center/pallas_call | solution.py:669
  27.3 2.8 %second.1 = (f32[16,32,1024]{2,1,0:T(8,128)}, f32[16,32,1024]{2,1,0:T(8,128)}, f32[2,2,16,8,1024]{4,3,2,1,0:T(8,128)S(1)}, f32[3,32,1024]{2,1,0:T(8,128)S(1)}, f...) custom-call(f32[8,8,128]{2,1,0:T(8,128)S(1)} %get-tuple-element.45.v, ...), custom_call_target="tpu_custom_call" | custom-call | flops 33554432 | bytes 65536 | tf_op jit(solution)/shard_map/second/pallas_call | solution.py:703
  30.1 0.0 collective-permute-done.3.p_high
  30.1 0.8 %rim.1 = (f32[2,2,32,1024]{3,2,1,0:T(8,128)S(1)}, f32[2,2,32,1024]{3,2,1,0:T(8,128)S(1)}, f32[3,32,1024]{2,1,0:T(8,128)S(1)}) custom-call(f32[8,8,128]{2,1,0:T(8,128)S(1)} %get-tuple-element.45.values, f32[2,32,1024]{2,1,0:T(8,128)S(1)} %collective-permute-done.2.p_low, f32[2,32,1024]{2,1,0:T(8,128)S(1)} %collective-permute-done.3.p_high, ...), custom_call_target="tpu_custom_call" | custom-call | flops 8388608 | bytes 65536 | tf_op jit(solution)/shard_map/rim/pallas_call | solution.py:728
  30.9 0.0 collective-permute-done.4.q_low
  31.0 0.0 collective-permute-done.5.q_high
  31.0 0.0 collective-permute-done.6.r_low
  31.0 1.1 %collective-permute-done.7.r_high = f32[2,16,768]{2,1,0:T(8,128)S(1)} collective-permute-done((f32[2,16,768]{2,1,0:T(8,128)S(1)}, f32[2,16,768]{2,1,0:T(8,128)S(1)}, u32[]{:S(2)}, u32[]{:S(2)}) %collective-permute-start.7) | collective-permute-done | bytes 98336 | tf_op jit(solution)/shard_map/ppermute | solution.py:612
  32.1 0.2 others.1
  32.2 1.5 %collective-permute-start.10 = (f32[3,32,256]{2,1,0:T(8,128)S(1)}, f32[3,32,256]{2,1,0:T(8,128)S(1)}, u32[]{:S(2)}, u32[]{:S(2)}) collective-permute-start(f32[3,32,256]{2,1,0:T(8,128)S(1)} %get-tuple-element.84), channel_id=1, source_target_pairs={{0,8},{8,0},{16,24},{24,16},{1,9},{9,1},{17,25},{25,17},{2,10},{10... | collective-permute-start | bytes 294920 | tf_op jit(solution)/shard_map/ppermute | solution.py:740
  33.8 0.5 %collective-permute-start.11 = (f32[3,32,256]{2,1,0:T(8,128)S(1)}, f32[3,32,256]{2,1,0:T(8,128)S(1)}, u32[]{:S(2)}, u32[]{:S(2)}) collective-permute-start(f32[3,32,256]{2,1,0:T(8,128)S(1)} %get-tuple-element.85), channel_id=1, source_target_pairs={{0,16},{8,24},{16,0},{24,8},{1,17},{9,25},{17,1},{25,9},{2,18},{10... | collective-permute-start | bytes 294920 | tf_op jit(solution)/shard_map/ppermute | solution.py:740
  34.3 1.5 %collective-permute-start.12 = (f32[3,32,256]{2,1,0:T(8,128)S(1)}, f32[3,32,256]{2,1,0:T(8,128)S(1)}, u32[]{:S(2)}, u32[]{:S(2)}) collective-permute-start(f32[3,32,256]{2,1,0:T(8,128)S(1)} %get-tuple-element.86), channel_id=1, source_target_pairs={{0,24},{8,16},{16,8},{24,0},{1,25},{9,17},{17,9},{25,1},{2,26},{10... | collective-permute-start | bytes 294920 | tf_op jit(solution)/shard_map/ppermute | solution.py:740
  35.8 1.5 %collective-permute-start.8 = (f32[2,32,256]{2,1,0:T(8,128)S(1)}, f32[2,32,256]{2,1,0:T(8,128)S(1)}, u32[]{:S(2)}, u32[]{:S(2)}) collective-permute-start(f32[2,32,256]{2,1,0:T(8,128)S(1)} %get-tuple-element.76), channel_id=1, source_target_pairs={{0,8},{8,16},{16,24},{24,0},{1,9},{9,17},{17,25},{25,1},{2,10},{10... | collective-permute-start | bytes 196616 | tf_op jit(solution)/shard_map/ppermute | solution.py:612
  37.3 1.4 %collective-permute-start.9 = (f32[2,32,256]{2,1,0:T(8,128)S(1)}, f32[2,32,256]{2,1,0:T(8,128)S(1)}, u32[]{:S(2)}, u32[]{:S(2)}) collective-permute-start(f32[2,32,256]{2,1,0:T(8,128)S(1)} %get-tuple-element.77), channel_id=1, source_target_pairs={{0,24},{8,0},{16,8},{24,16},{1,25},{9,1},{17,9},{25,17},{2,26},{10... | collective-permute-start | bytes 196616 | tf_op jit(solution)/shard_map/ppermute | solution.py:612
  38.7 2.2 %collective-permute-done.8.o_low = f32[2,32,256]{2,1,0:T(8,128)S(1)} collective-permute-done((f32[2,32,256]{2,1,0:T(8,128)S(1)}, f32[2,32,256]{2,1,0:T(8,128)S(1)}, u32[]{:S(2)}, u32[]{:S(2)}) %collective-permute-start.8) | collective-permute-done | bytes 65568 | tf_op jit(solution)/shard_map/ppermute | solution.py:612
  40.9 0.6 %collective-permute-done.9.o_high = f32[2,32,256]{2,1,0:T(8,128)S(1)} collective-permute-done((f32[2,32,256]{2,1,0:T(8,128)S(1)}, f32[2,32,256]{2,1,0:T(8,128)S(1)}, u32[]{:S(2)}, u32[]{:S(2)}) %collective-permute-start.9) | collective-permute-done | bytes 65568 | tf_op jit(solution)/shard_map/ppermute | solution.py:612
  41.5 0.1 own.1
  41.6 1.7 %put.1 = (f32[16,32,1024]{2,1,0:T(8,128)}, f32[16,32,1024]{2,1,0:T(8,128)}) custom-call(f32[2,2,16,8,1024]{4,3,2,1,0:T(8,128)S(1)} %get-tuple-element.55.new, f32[2,2,32,1024]{3,2,1,0:T(8,128)S(1)} %get-tuple-element.66.ring, f32[2,2,32,1024]{3,2,1,0:T(8,128)S(1)} %get-tuple-element.75.others, ...), custom_call_target="tpu_custom_call", output_to_operand_aliasing={{0}: (4, {}), {1}: (5, {})} | custom-call | flops 4194304 | bytes 65536 | tf_op jit(solution)/shard_map/put/pallas_call | solution.py:765
  43.3 0.0 collective-permute-done.10.pieces_and_rest_1_
  43.3 0.0 collective-permute-done.11.pieces_and_rest_2_
  43.3 0.0 collective-permute-done.12.pieces_and_rest_3_
  43.3 0.7 %paint.1 = f32[4,32,256]{2,1,0:T(8,128)} custom-call(f32[8,8,128]{2,1,0:T(8,128)S(1)} %get-tuple-element.45.values, f32[3,32,256]{2,1,0:T(8,128)S(1)} %get-tuple-element.83.pieces_and_rest_0_, f32[3,32,256]{2,1,0:T(8,128)S(1)} %collective-permute-done.10.pieces_and_rest_1_, f32[3,32,256]{2,1,0:T(8,128)S(1)} %collective-permute-done.11.pieces_and_rest_2_, ...), custom_call_target="tpu_custom_call" | custom-call | flops 1048576 | bytes 65536 | tf_op jit(solution)/shard_map/paint/pallas_call | solution.py:776
  (3 shorter events, 0.1 us)
Async XLA Ops:
  0.6 1.6 %copy-start = (f32[16,32,1024]{2,1,0:T(8,128)S(1)}, f32[16,32,1024]{2,1,0:T(8,128)}, u32[]{:S(2)}) copy-start(f32[16,32,1024]{2,1,0:T(8,128)} %sub.5) | copy-start | bytes 6291460
  2.2 1.6 %copy-start.2 = (f32[16,32,1024]{2,1,0:T(8,128)S(1)}, f32[16,32,1024]{2,1,0:T(8,128)}, u32[]{:S(2)}) copy-start(f32[16,32,1024]{2,1,0:T(8,128)} %cat.5) | copy-start | bytes 6291460
  4.3 9.9 %collective-permute-start = (f32[2,2,16,1024]{3,2,1,0:T(8,128)S(1)}, f32[2,2,16,1024]{3,2,1,0:T(8,128)S(1)}, u32[]{:S(2)}, u32[]{:S(2)}) collective-permute-start(f32[2,2,16,1024]{3,2,1,0:T(8,128)S(1)} %get-tuple-element.51.own_high), channel_id=1, source_target_pairs={{0,1},{1,2},{2,3},{3,4},{4,5},{5,6},{6,7},{7,0},{8,9},{9,10},{10,1... | collective-permute-start | bytes 786440 | tf_op jit(solution)/shard_map/ppermute | solution.py:612
  4.8 17.3 %copy-start.1 = (f32[16,32,1024]{2,1,0:T(8,128)S(1)}, f32[16,32,1024]{2,1,0:T(8,128)}, u32[]{:S(2)}) copy-start(f32[16,32,1024]{2,1,0:T(8,128)} %sub.5) | copy-start | bytes 6291460
  4.8 17.3 %copy-start.3 = (f32[16,32,1024]{2,1,0:T(8,128)S(1)}, f32[16,32,1024]{2,1,0:T(8,128)}, u32[]{:S(2)}) copy-start(f32[16,32,1024]{2,1,0:T(8,128)} %cat.5) | copy-start | bytes 6291460
  4.8 11.7 %collective-permute-start.1 = (f32[2,2,16,1024]{3,2,1,0:T(8,128)S(1)}, f32[2,2,16,1024]{3,2,1,0:T(8,128)S(1)}, u32[]{:S(2)}, u32[]{:S(2)}) collective-permute-start(f32[2,2,16,1024]{3,2,1,0:T(8,128)S(1)} %get-tuple-element.52.own_low), channel_id=1, source_target_pairs={{0,7},{1,0},{2,1},{3,2},{4,3},{5,4},{6,5},{7,6},{8,15},{9,8},{10,9... | collective-permute-start | bytes 786440 | tf_op jit(solution)/shard_map/ppermute | solution.py:612
  10.1 10.1 %collective-permute-start.2 = (f32[2,32,1024]{2,1,0:T(8,128)S(1)}, f32[2,32,1024]{2,1,0:T(8,128)S(1)}, u32[]{:S(2)}, u32[]{:S(2)}) collective-permute-start(f32[2,32,1024]{2,1,0:T(8,128)S(1)} %get-tuple-element.56.up), channel_id=1, source_target_pairs={{0,8},{8,16},{16,24},{24,0},{1,9},{9,17},{17,25},{25,1},{2,10},{10... | collective-permute-start | bytes 786440 | tf_op jit(solution)/shard_map/ppermute | solution.py:612
  12.0 18.1 %collective-permute-start.3 = (f32[2,32,1024]{2,1,0:T(8,128)S(1)}, f32[2,32,1024]{2,1,0:T(8,128)S(1)}, u32[]{:S(2)}, u32[]{:S(2)}) collective-permute-start(f32[2,32,1024]{2,1,0:T(8,128)S(1)} %get-tuple-element.57.down), channel_id=1, source_target_pairs={{0,24},{8,0},{16,8},{24,16},{1,25},{9,1},{17,9},{25,17},{2,26},{10... | collective-permute-start | bytes 786440 | tf_op jit(solution)/shard_map/ppermute | solution.py:612
  13.1 17.9 %collective-permute-start.4 = (f32[2,16,768]{2,1,0:T(8,128)S(1)}, f32[2,16,768]{2,1,0:T(8,128)S(1)}, u32[]{:S(2)}, u32[]{:S(2)}) collective-permute-start(f32[2,16,768]{2,1,0:T(8,128)S(1)} %get-tuple-element.68), channel_id=1, source_target_pairs={{0,8},{8,16},{16,24},{24,0},{1,9},{9,17},{17,25},{25,1},{2,10},{10... | collective-permute-start | bytes 294920 | tf_op jit(solution)/shard_map/ppermute | solution.py:612
  14.1 16.8 %collective-permute-start.5 = (f32[2,16,768]{2,1,0:T(8,128)S(1)}, f32[2,16,768]{2,1,0:T(8,128)S(1)}, u32[]{:S(2)}, u32[]{:S(2)}) collective-permute-start(f32[2,16,768]{2,1,0:T(8,128)S(1)} %get-tuple-element.69), channel_id=1, source_target_pairs={{0,24},{8,0},{16,8},{24,16},{1,25},{9,1},{17,9},{25,17},{2,26},{10... | collective-permute-start | bytes 294920 | tf_op jit(solution)/shard_map/ppermute | solution.py:612
  16.7 14.3 %collective-permute-start.6 = (f32[2,16,768]{2,1,0:T(8,128)S(1)}, f32[2,16,768]{2,1,0:T(8,128)S(1)}, u32[]{:S(2)}, u32[]{:S(2)}) collective-permute-start(f32[2,16,768]{2,1,0:T(8,128)S(1)} %get-tuple-element.72), channel_id=1, source_target_pairs={{0,8},{8,16},{16,24},{24,0},{1,9},{9,17},{17,25},{25,1},{2,10},{10... | collective-permute-start | bytes 294920 | tf_op jit(solution)/shard_map/ppermute | solution.py:612
  20.2 11.9 %collective-permute-start.7 = (f32[2,16,768]{2,1,0:T(8,128)S(1)}, f32[2,16,768]{2,1,0:T(8,128)S(1)}, u32[]{:S(2)}, u32[]{:S(2)}) collective-permute-start(f32[2,16,768]{2,1,0:T(8,128)S(1)} %get-tuple-element.73), channel_id=1, source_target_pairs={{0,24},{8,0},{16,8},{24,16},{1,25},{9,1},{17,9},{25,17},{2,26},{10... | collective-permute-start | bytes 294920 | tf_op jit(solution)/shard_map/ppermute | solution.py:612
  32.2 11.0 %collective-permute-start.10 = (f32[3,32,256]{2,1,0:T(8,128)S(1)}, f32[3,32,256]{2,1,0:T(8,128)S(1)}, u32[]{:S(2)}, u32[]{:S(2)}) collective-permute-start(f32[3,32,256]{2,1,0:T(8,128)S(1)} %get-tuple-element.84), channel_id=1, source_target_pairs={{0,8},{8,0},{16,24},{24,16},{1,9},{9,1},{17,25},{25,17},{2,10},{10... | collective-permute-start | bytes 294920 | tf_op jit(solution)/shard_map/ppermute | solution.py:740
  33.8 9.5 %collective-permute-start.11 = (f32[3,32,256]{2,1,0:T(8,128)S(1)}, f32[3,32,256]{2,1,0:T(8,128)S(1)}, u32[]{:S(2)}, u32[]{:S(2)}) collective-permute-start(f32[3,32,256]{2,1,0:T(8,128)S(1)} %get-tuple-element.85), channel_id=1, source_target_pairs={{0,16},{8,24},{16,0},{24,8},{1,17},{9,25},{17,1},{25,9},{2,18},{10... | collective-permute-start | bytes 294920 | tf_op jit(solution)/shard_map/ppermute | solution.py:740
  34.3 9.0 %collective-permute-start.12 = (f32[3,32,256]{2,1,0:T(8,128)S(1)}, f32[3,32,256]{2,1,0:T(8,128)S(1)}, u32[]{:S(2)}, u32[]{:S(2)}) collective-permute-start(f32[3,32,256]{2,1,0:T(8,128)S(1)} %get-tuple-element.86), channel_id=1, source_target_pairs={{0,24},{8,16},{16,8},{24,0},{1,25},{9,17},{17,9},{25,1},{2,26},{10... | collective-permute-start | bytes 294920 | tf_op jit(solution)/shard_map/ppermute | solution.py:740
  35.8 5.2 %collective-permute-start.8 = (f32[2,32,256]{2,1,0:T(8,128)S(1)}, f32[2,32,256]{2,1,0:T(8,128)S(1)}, u32[]{:S(2)}, u32[]{:S(2)}) collective-permute-start(f32[2,32,256]{2,1,0:T(8,128)S(1)} %get-tuple-element.76), channel_id=1, source_target_pairs={{0,8},{8,16},{16,24},{24,0},{1,9},{9,17},{17,25},{25,1},{2,10},{10... | collective-permute-start | bytes 196616 | tf_op jit(solution)/shard_map/ppermute | solution.py:612
  37.3 4.3 %collective-permute-start.9 = (f32[2,32,256]{2,1,0:T(8,128)S(1)}, f32[2,32,256]{2,1,0:T(8,128)S(1)}, u32[]{:S(2)}, u32[]{:S(2)}) collective-permute-start(f32[2,32,256]{2,1,0:T(8,128)S(1)} %get-tuple-element.77), channel_id=1, source_target_pairs={{0,24},{8,0},{16,8},{24,16},{1,25},{9,1},{17,9},{25,17},{2,26},{10... | collective-permute-start | bytes 196616 | tf_op jit(solution)/shard_map/ppermute | solution.py:612
where the time goes:
time: 44.2 us; the launch traced here: 44 us
  starting transfers between devices  19.6 us (44%)
  Pallas kernels  13 us (29%)
  waiting for transfers between devices  7.4 us (17%)
  local copies, waits for them, and re-layouts  3.18 us (7%)
  between operations  0.79 us (2%)
    ppermute x10, starting transfers between devices, shifted(): return lax.ppermute(x, axis, ring(lax.axis_size(axis), shift))  16.1 us
    ppermute x10, waiting for transfers between devices, shifted(): return lax.ppermute(x, axis, ring(lax.axis_size(axis), shift))  7.4 us
    ppermute x3, starting transfers between devices, paired(): lax.ppermute(piece, 'gz', [(i, int(partner(i, shift, count))) for i in ra...  3.55 us
    unnamed x8, local copies, waits for them, and re-layouts  3.18 us
    pallas_call x1, Pallas kernels, body(): call(functools.partial(first_kernel, share), 1 << 24, 2, name='first', ou...  3 us
    pallas_call x1, Pallas kernels, body(): call(second_kernel, 1 << 25, 4, name='second', out_shape=(f32(depth, rows...  2.84 us
    pallas_call x1, Pallas kernels, body(): call(center_kernel, 1 << 24, 2, name='center', out_shape=(f32(2, depth, m...  2.06 us
    pallas_call x1, Pallas kernels, body(): call(functools.partial(put_kernel, count), 1 << 22, 2, name='put', out_sh...  1.68 us
  transfers between devices with their start and end apart: 13, of which 4 were waited for; matrix products, arithmetic and copies ran while one was open for 0% of the time, Pallas kernels for 27%

commit v1 on v0

--- a/solution.py
+++ b/solution.py
@@ -525,16 +525,17 @@
 
 
 def paint_kernel(values, *pieces_and_rest):
-    *pieces, image, slabs = pieces_and_rest
+    *pieces, out, slabs, image, sems = pieces_and_rest
     count = len(pieces)
     me = lax.axis_index("gz")
     for shift, piece in enumerate(pieces):
         slabs[origin(me, shift, count)] = piece[...]
-    shade(values, slabs, image, count)
-
-
-def shade(values, slabs, image, count):
+    shade(values, slabs, out, image, sems, count)
+
+
+def shade(values, slabs, out, image, sems, count):
     rows, wide = image.shape[1:]
+    copies = []
     for tile in range(rows // ROWS):
         at = span(tile)
         sub, cat, clear = slabs[0, 0, at, :], slabs[0, 1, at, :], slabs[0, 2, at, :]
@@ -547,10 +548,14 @@
             of_cat = across_columns(values[3 + channel * 2], wide)
             image[channel, at, :] = of_sub * sub + of_cat * cat
         image[3, at, :] = 1.0 - clear
+        copies.append(pltpu.make_async_copy(image.at[:, at], out.at[:, at], sems.at[tile]))
+        copies[-1].start()
+    for copy in copies:
+        copy.wait()
 
 
 def shade_kernel(values, half, *pieces_and_rest):
-    *pieces, image, slabs = pieces_and_rest
+    *pieces, out, slabs, image, sems = pieces_and_rest
     count = len(pieces)
     rows, _ = image.shape[1:]
     me = lax.axis_index("gz")
@@ -562,7 +567,7 @@
             slabs[slab, :, pl.ds(ROWS, rows - 2 * ROWS), :] = half[...]
             slabs[slab, :, span(0), :] = piece[:, :ROWS]
             slabs[slab, :, pl.ds(rows - ROWS, ROWS), :] = piece[:, ROWS:]
-    shade(values, slabs, image, count)
+    shade(values, slabs, out, image, sems, count)
 
 
 def place_kernel(new, ring, inner, outer, sub_in, cat_in, sub_out, cat_out, sems):
@@ -780,8 +785,12 @@
             name="paint",
             out_shape=f32(4, rows, wide),
             in_specs=[VMEM] * (1 + count),
-            out_specs=VMEM,
-            scratch_shapes=[pltpu.VMEM((count, 3, rows, wide), jnp.float32)],
+            out_specs=HBM,
+            scratch_shapes=[
+                pltpu.VMEM((count, 3, rows, wide), jnp.float32),
+                pltpu.VMEM((4, rows, wide), jnp.float32),
+                pltpu.SemaphoreType.DMA((rows // ROWS,)),
+            ],
         )(values, *received)
         return sub_final, cat_final, image
 
@@ -833,8 +842,12 @@
         name="shade",
         out_shape=f32(4, rows, wide),
         in_specs=[VMEM] * (2 + count),
-        out_specs=VMEM,
-        scratch_shapes=[pltpu.VMEM((count, 3, rows, wide), jnp.float32)],
+        out_specs=HBM,
+        scratch_shapes=[
+            pltpu.VMEM((count, 3, rows, wide), jnp.float32),
+            pltpu.VMEM((4, rows, wide), jnp.float32),
+            pltpu.SemaphoreType.DMA((rows // ROWS,)),
+        ],
     )(values, half_piece, *received)
     return sub_final, cat_final, image
 

time: 44.2 us -> 44.2 us (level)
  no operation moved by 1% of the time
where the time goes in v1:
time: 44.2 us; the launch traced here: 44 us
  starting transfers between devices  19.6 us (44%)
  Pallas kernels  13 us (29%)
  waiting for transfers between devices  7.4 us (17%)
  local copies, waits for them, and re-layouts  3.18 us (7%)
  between operations  0.79 us (2%)
    ppermute x10, starting transfers between devices, shifted(): return lax.ppermute(x, axis, ring(lax.axis_size(axis), shift))  16.1 us
    ppermute x10, waiting for transfers between devices, shifted(): return lax.ppermute(x, axis, ring(lax.axis_size(axis), shift))  7.4 us
    ppermute x3, starting transfers between devices, paired(): lax.ppermute(piece, 'gz', [(i, int(partner(i, shift, count))) for i in ra...  3.55 us
    unnamed x8, local copies, waits for them, and re-layouts  3.18 us
    pallas_call x1, Pallas kernels, body(): call(functools.partial(first_kernel, share), 1 << 24, 2, name='first', ou...  3 us
    pallas_call x1, Pallas kernels, body(): call(second_kernel, 1 << 25, 4, name='second', out_shape=(f32(depth, rows...  2.84 us
    pallas_call x1, Pallas kernels, body(): call(center_kernel, 1 << 24, 2, name='center', out_shape=(f32(2, depth, m...  2.06 us
    pallas_call x1, Pallas kernels, body(): call(functools.partial(put_kernel, count), 1 << 22, 2, name='put', out_sh...  1.68 us
  transfers between devices with their start and end apart: 13, of which 4 were waited for; matrix products, arithmetic and copies ran while one was open for 0% of the time, Pallas kernels for 27%

profile of v1, /device:TPU:0, one launch (start us, length us, event | category | flops | bytes accessed | tf_op | source)
XLA Modules:
  0.0 44.0 jit_solution(18399843952478079871)
XLA Ops:
  0.6 0.0 copy-start
  0.6 1.6 %copy-done = f32[16,32,1024]{2,1,0:T(8,128)S(1)} copy-done((f32[16,32,1024]{2,1,0:T(8,128)S(1)}, f32[16,32,1024]{2,1,0:T(8,128)}, u32[]{:S(2)}) %copy-start) | copy-done | bytes 2097176
  2.2 0.0 copy-start.2
  2.2 1.6 %copy-done.2 = f32[16,32,1024]{2,1,0:T(8,128)S(1)} copy-done((f32[16,32,1024]{2,1,0:T(8,128)S(1)}, f32[16,32,1024]{2,1,0:T(8,128)}, u32[]{:S(2)}) %copy-start.2) | copy-done | bytes 2097176
  3.8 0.5 %prepare.1 = (f32[2,2,16,1024]{3,2,1,0:T(8,128)S(1)}, f32[2,2,16,1024]{3,2,1,0:T(8,128)S(1)}, f32[2,16,1024]{2,1,0:T(8,128)S(1)}, f32[2,16,1024]{2,1,0:T(8,128)S...) custom-call(f32[16,32,1024]{2,1,0:T(8,128)S(1)} %copy-done, f32[16,32,1024]{2,1,0:T(8,128)S(1)} %copy-done.2), custom_call_target="tpu_custom_call" | custom-call | flops 4194304 | bytes 65536 | tf_op jit(solution)/shard_map/prepare/pallas_call | solution.py:632
  4.3 0.5 %collective-permute-start = (f32[2,2,16,1024]{3,2,1,0:T(8,128)S(1)}, f32[2,2,16,1024]{3,2,1,0:T(8,128)S(1)}, u32[]{:S(2)}, u32[]{:S(2)}) collective-permute-start(f32[2,2,16,1024]{3,2,1,0:T(8,128)S(1)} %get-tuple-element.51.own_high), channel_id=1, source_target_pairs={{0,1},{1,2},{2,3},{3,4},{4,5},{5,6},{6,7},{7,0},{8,9},{9,10},{10,1... | collective-permute-start | bytes 786440 | tf_op jit(solution)/shard_map/ppermute | solution.py:617
  4.8 0.0 copy-start.1
  4.8 0.0 copy-start.3
  4.8 4.1 %collective-permute-start.1 = (f32[2,2,16,1024]{3,2,1,0:T(8,128)S(1)}, f32[2,2,16,1024]{3,2,1,0:T(8,128)S(1)}, u32[]{:S(2)}, u32[]{:S(2)}) collective-permute-start(f32[2,2,16,1024]{3,2,1,0:T(8,128)S(1)} %get-tuple-element.52.own_low), channel_id=1, source_target_pairs={{0,7},{1,0},{2,1},{3,2},{4,3},{5,4},{6,5},{7,6},{8,15},{9,8},{10,9... | collective-permute-start | bytes 786440 | tf_op jit(solution)/shard_map/ppermute | solution.py:617
  8.9 1.1 %planes.1 = (f32[2,32,1024]{2,1,0:T(8,128)S(1)}, f32[2,32,1024]{2,1,0:T(8,128)S(1)}) custom-call(f32[16,32,1024]{2,1,0:T(8,128)} %sub.5, f32[16,32,1024]{2,1,0:T(8,128)} %cat.5), custom_call_target="tpu_custom_call" | custom-call | flops 1048576 | bytes 65536 | tf_op jit(solution)/shard_map/planes/pallas_call | solution.py:619
  10.1 2.0 %collective-permute-start.2 = (f32[2,32,1024]{2,1,0:T(8,128)S(1)}, f32[2,32,1024]{2,1,0:T(8,128)S(1)}, u32[]{:S(2)}, u32[]{:S(2)}) collective-permute-start(f32[2,32,1024]{2,1,0:T(8,128)S(1)} %get-tuple-element.56.up), channel_id=1, source_target_pairs={{0,8},{8,16},{16,24},{24,0},{1,9},{9,17},{17,25},{25,1},{2,10},{10... | collective-permute-start | bytes 786440 | tf_op jit(solution)/shard_map/ppermute | solution.py:617
  12.0 1.0 %collective-permute-start.3 = (f32[2,32,1024]{2,1,0:T(8,128)S(1)}, f32[2,32,1024]{2,1,0:T(8,128)S(1)}, u32[]{:S(2)}, u32[]{:S(2)}) collective-permute-start(f32[2,32,1024]{2,1,0:T(8,128)S(1)} %get-tuple-element.57.down), channel_id=1, source_target_pairs={{0,24},{8,0},{16,8},{24,16},{1,25},{9,1},{17,9},{25,17},{2,26},{10... | collective-permute-start | bytes 786440 | tf_op jit(solution)/shard_map/ppermute | solution.py:617
  13.1 1.1 %collective-permute-start.4 = (f32[2,16,768]{2,1,0:T(8,128)S(1)}, f32[2,16,768]{2,1,0:T(8,128)S(1)}, u32[]{:S(2)}, u32[]{:S(2)}) collective-permute-start(f32[2,16,768]{2,1,0:T(8,128)S(1)} %get-tuple-element.68), channel_id=1, source_target_pairs={{0,8},{8,16},{16,24},{24,0},{1,9},{9,17},{17,25},{25,1},{2,10},{10... | collective-permute-start | bytes 294920 | tf_op jit(solution)/shard_map/ppermute | solution.py:617
  14.1 0.0 collective-permute-done.from_low
  14.1 2.4 %collective-permute-start.5 = (f32[2,16,768]{2,1,0:T(8,128)S(1)}, f32[2,16,768]{2,1,0:T(8,128)S(1)}, u32[]{:S(2)}, u32[]{:S(2)}) collective-permute-start(f32[2,16,768]{2,1,0:T(8,128)S(1)} %get-tuple-element.69), channel_id=1, source_target_pairs={{0,24},{8,0},{16,8},{24,16},{1,25},{9,1},{17,9},{25,17},{2,26},{10... | collective-permute-start | bytes 294920 | tf_op jit(solution)/shard_map/ppermute | solution.py:617
  16.6 0.0 collective-permute-done.1.from_high
  16.7 0.1 collective-permute-start.6
  16.7 3.5 %collective-permute-done.2.p_low = f32[2,32,1024]{2,1,0:T(8,128)S(1)} collective-permute-done((f32[2,32,1024]{2,1,0:T(8,128)S(1)}, f32[2,32,1024]{2,1,0:T(8,128)S(1)}, u32[]{:S(2)}, u32[]{:S(2)}) %collective-permute-start.2) | collective-permute-done | bytes 262176 | tf_op jit(solution)/shard_map/ppermute | solution.py:617
  20.2 2.0 %collective-permute-start.7 = (f32[2,16,768]{2,1,0:T(8,128)S(1)}, f32[2,16,768]{2,1,0:T(8,128)S(1)}, u32[]{:S(2)}, u32[]{:S(2)}) collective-permute-start(f32[2,16,768]{2,1,0:T(8,128)S(1)} %get-tuple-element.73), channel_id=1, source_target_pairs={{0,24},{8,0},{16,8},{24,16},{1,25},{9,1},{17,9},{25,17},{2,26},{10... | collective-permute-start | bytes 294920 | tf_op jit(solution)/shard_map/ppermute | solution.py:617
  22.2 0.0 copy-done.1
  22.2 0.0 copy-done.3
  22.2 3.0 %first.1 = (f32[2,16,32,1024]{3,2,1,0:T(8,128)S(1)}, f32[8,8,128]{2,1,0:T(8,128)S(1)}) custom-call(f32[2]{0:T(128)} %scale_hbm.1, f32[2,3]{1,0:T(2,128)} %bitcast.1, f32[16,32,1024]{2,1,0:T(8,128)S(1)} %copy-done.1, f32[16,32,1024]{2,1,0:T(8,128)S(1)} %copy-done.3), custom_call_target="tpu_custom_call" | custom-call | flops 16777216 | bytes 65536 | tf_op jit(solution)/shard_map/first/pallas_call | solution.py:660
  25.2 2.1 %center.1 = (f32[2,16,16,1024]{3,2,1,0:T(8,128)S(1)}, f32[3,32,1024]{2,1,0:T(8,128)S(1)}) custom-call(f32[8,8,128]{2,1,0:T(8,128)S(1)} %get-tuple-element.45.values, f32[2,16,32,1024]{3,2,1,0:T(8,128)S(1)} %get-tuple-element.46.mid), custom_call_target="tpu_custom_call" | custom-call | flops 16777216 | bytes 65536 | tf_op jit(solution)/shard_map/center/pallas_call | solution.py:674
  27.3 2.8 %second.1 = (f32[16,32,1024]{2,1,0:T(8,128)}, f32[16,32,1024]{2,1,0:T(8,128)}, f32[2,2,16,8,1024]{4,3,2,1,0:T(8,128)S(1)}, f32[3,32,1024]{2,1,0:T(8,128)S(1)}, f...) custom-call(f32[8,8,128]{2,1,0:T(8,128)S(1)} %get-tuple-element.45.v, ...), custom_call_target="tpu_custom_call" | custom-call | flops 33554432 | bytes 65536 | tf_op jit(solution)/shard_map/second/pallas_call | solution.py:708
  30.1 0.0 collective-permute-done.3.p_high
  30.1 0.8 %rim.1 = (f32[2,2,32,1024]{3,2,1,0:T(8,128)S(1)}, f32[2,2,32,1024]{3,2,1,0:T(8,128)S(1)}, f32[3,32,1024]{2,1,0:T(8,128)S(1)}) custom-call(f32[8,8,128]{2,1,0:T(8,128)S(1)} %get-tuple-element.45.values, f32[2,32,1024]{2,1,0:T(8,128)S(1)} %collective-permute-done.2.p_low, f32[2,32,1024]{2,1,0:T(8,128)S(1)} %collective-permute-done.3.p_high, ...), custom_call_target="tpu_custom_call" | custom-call | flops 8388608 | bytes 65536 | tf_op jit(solution)/shard_map/rim/pallas_call | solution.py:733
  30.9 0.0 collective-permute-done.4.q_low
  31.0 0.0 collective-permute-done.5.q_high
  31.0 0.0 collective-permute-done.6.r_low
  31.0 1.1 %collective-permute-done.7.r_high = f32[2,16,768]{2,1,0:T(8,128)S(1)} collective-permute-done((f32[2,16,768]{2,1,0:T(8,128)S(1)}, f32[2,16,768]{2,1,0:T(8,128)S(1)}, u32[]{:S(2)}, u32[]{:S(2)}) %collective-permute-start.7) | collective-permute-done | bytes 98336 | tf_op jit(solution)/shard_map/ppermute | solution.py:617
  32.1 0.2 others.1
  32.2 1.5 %collective-permute-start.10 = (f32[3,32,256]{2,1,0:T(8,128)S(1)}, f32[3,32,256]{2,1,0:T(8,128)S(1)}, u32[]{:S(2)}, u32[]{:S(2)}) collective-permute-start(f32[3,32,256]{2,1,0:T(8,128)S(1)} %get-tuple-element.84), channel_id=1, source_target_pairs={{0,8},{8,0},{16,24},{24,16},{1,9},{9,1},{17,25},{25,17},{2,10},{10... | collective-permute-start | bytes 294920 | tf_op jit(solution)/shard_map/ppermute | solution.py:745
  33.8 0.5 %collective-permute-start.11 = (f32[3,32,256]{2,1,0:T(8,128)S(1)}, f32[3,32,256]{2,1,0:T(8,128)S(1)}, u32[]{:S(2)}, u32[]{:S(2)}) collective-permute-start(f32[3,32,256]{2,1,0:T(8,128)S(1)} %get-tuple-element.85), channel_id=1, source_target_pairs={{0,16},{8,24},{16,0},{24,8},{1,17},{9,25},{17,1},{25,9},{2,18},{10... | collective-permute-start | bytes 294920 | tf_op jit(solution)/shard_map/ppermute | solution.py:745
  34.3 1.5 %collective-permute-start.12 = (f32[3,32,256]{2,1,0:T(8,128)S(1)}, f32[3,32,256]{2,1,0:T(8,128)S(1)}, u32[]{:S(2)}, u32[]{:S(2)}) collective-permute-start(f32[3,32,256]{2,1,0:T(8,128)S(1)} %get-tuple-element.86), channel_id=1, source_target_pairs={{0,24},{8,16},{16,8},{24,0},{1,25},{9,17},{17,9},{25,1},{2,26},{10... | collective-permute-start | bytes 294920 | tf_op jit(solution)/shard_map/ppermute | solution.py:745
  35.8 1.5 %collective-permute-start.8 = (f32[2,32,256]{2,1,0:T(8,128)S(1)}, f32[2,32,256]{2,1,0:T(8,128)S(1)}, u32[]{:S(2)}, u32[]{:S(2)}) collective-permute-start(f32[2,32,256]{2,1,0:T(8,128)S(1)} %get-tuple-element.76), channel_id=1, source_target_pairs={{0,8},{8,16},{16,24},{24,0},{1,9},{9,17},{17,25},{25,1},{2,10},{10... | collective-permute-start | bytes 196616 | tf_op jit(solution)/shard_map/ppermute | solution.py:617
  37.3 1.4 %collective-permute-start.9 = (f32[2,32,256]{2,1,0:T(8,128)S(1)}, f32[2,32,256]{2,1,0:T(8,128)S(1)}, u32[]{:S(2)}, u32[]{:S(2)}) collective-permute-start(f32[2,32,256]{2,1,0:T(8,128)S(1)} %get-tuple-element.77), channel_id=1, source_target_pairs={{0,24},{8,0},{16,8},{24,16},{1,25},{9,1},{17,9},{25,17},{2,26},{10... | collective-permute-start | bytes 196616 | tf_op jit(solution)/shard_map/ppermute | solution.py:617
  38.7 2.2 %collective-permute-done.8.o_low = f32[2,32,256]{2,1,0:T(8,128)S(1)} collective-permute-done((f32[2,32,256]{2,1,0:T(8,128)S(1)}, f32[2,32,256]{2,1,0:T(8,128)S(1)}, u32[]{:S(2)}, u32[]{:S(2)}) %collective-permute-start.8) | collective-permute-done | bytes 65568 | tf_op jit(solution)/shard_map/ppermute | solution.py:617
  40.9 0.6 %collective-permute-done.9.o_high = f32[2,32,256]{2,1,0:T(8,128)S(1)} collective-permute-done((f32[2,32,256]{2,1,0:T(8,128)S(1)}, f32[2,32,256]{2,1,0:T(8,128)S(1)}, u32[]{:S(2)}, u32[]{:S(2)}) %collective-permute-start.9) | collective-permute-done | bytes 65568 | tf_op jit(solution)/shard_map/ppermute | solution.py:617
  41.5 0.1 own.1
  41.6 1.7 %put.1 = (f32[16,32,1024]{2,1,0:T(8,128)}, f32[16,32,1024]{2,1,0:T(8,128)}) custom-call(f32[2,2,16,8,1024]{4,3,2,1,0:T(8,128)S(1)} %get-tuple-element.55.new, f32[2,2,32,1024]{3,2,1,0:T(8,128)S(1)} %get-tuple-element.66.ring, f32[2,2,32,1024]{3,2,1,0:T(8,128)S(1)} %get-tuple-element.75.others, ...), custom_call_target="tpu_custom_call", output_to_operand_aliasing={{0}: (4, {}), {1}: (5, {})} | custom-call | flops 4194304 | bytes 65536 | tf_op jit(solution)/shard_map/put/pallas_call | solution.py:770
  43.3 0.0 collective-permute-done.10.pieces_and_rest_1_
  43.3 0.0 collective-permute-done.11.pieces_and_rest_2_
  43.3 0.0 collective-permute-done.12.pieces_and_rest_3_
  43.3 0.7 %paint.1 = f32[4,32,256]{2,1,0:T(8,128)} custom-call(f32[8,8,128]{2,1,0:T(8,128)S(1)} %get-tuple-element.45.values, f32[3,32,256]{2,1,0:T(8,128)S(1)} %get-tuple-element.83.pieces_and_rest_0_, f32[3,32,256]{2,1,0:T(8,128)S(1)} %collective-permute-done.10.pieces_and_rest_1_, f32[3,32,256]{2,1,0:T(8,128)S(1)} %collective-permute-done.11.pieces_and_rest_2_, ...), custom_call_target="tpu_custom_call" | custom-call | flops 1048576 | bytes 65536 | tf_op jit(solution)/shard_map/paint/pallas_call | solution.py:781
  (3 shorter events, 0.1 us)
Async XLA Ops:
  0.6 1.6 %copy-start = (f32[16,32,1024]{2,1,0:T(8,128)S(1)}, f32[16,32,1024]{2,1,0:T(8,128)}, u32[]{:S(2)}) copy-start(f32[16,32,1024]{2,1,0:T(8,128)} %sub.5) | copy-start | bytes 6291460
  2.2 1.6 %copy-start.2 = (f32[16,32,1024]{2,1,0:T(8,128)S(1)}, f32[16,32,1024]{2,1,0:T(8,128)}, u32[]{:S(2)}) copy-start(f32[16,32,1024]{2,1,0:T(8,128)} %cat.5) | copy-start | bytes 6291460
  4.3 9.9 %collective-permute-start = (f32[2,2,16,1024]{3,2,1,0:T(8,128)S(1)}, f32[2,2,16,1024]{3,2,1,0:T(8,128)S(1)}, u32[]{:S(2)}, u32[]{:S(2)}) collective-permute-start(f32[2,2,16,1024]{3,2,1,0:T(8,128)S(1)} %get-tuple-element.51.own_high), channel_id=1, source_target_pairs={{0,1},{1,2},{2,3},{3,4},{4,5},{5,6},{6,7},{7,0},{8,9},{9,10},{10,1... | collective-permute-start | bytes 786440 | tf_op jit(solution)/shard_map/ppermute | solution.py:617
  4.8 17.3 %copy-start.1 = (f32[16,32,1024]{2,1,0:T(8,128)S(1)}, f32[16,32,1024]{2,1,0:T(8,128)}, u32[]{:S(2)}) copy-start(f32[16,32,1024]{2,1,0:T(8,128)} %sub.5) | copy-start | bytes 6291460
  4.8 17.3 %copy-start.3 = (f32[16,32,1024]{2,1,0:T(8,128)S(1)}, f32[16,32,1024]{2,1,0:T(8,128)}, u32[]{:S(2)}) copy-start(f32[16,32,1024]{2,1,0:T(8,128)} %cat.5) | copy-start | bytes 6291460
  4.8 11.7 %collective-permute-start.1 = (f32[2,2,16,1024]{3,2,1,0:T(8,128)S(1)}, f32[2,2,16,1024]{3,2,1,0:T(8,128)S(1)}, u32[]{:S(2)}, u32[]{:S(2)}) collective-permute-start(f32[2,2,16,1024]{3,2,1,0:T(8,128)S(1)} %get-tuple-element.52.own_low), channel_id=1, source_target_pairs={{0,7},{1,0},{2,1},{3,2},{4,3},{5,4},{6,5},{7,6},{8,15},{9,8},{10,9... | collective-permute-start | bytes 786440 | tf_op jit(solution)/shard_map/ppermute | solution.py:617
  10.1 10.1 %collective-permute-start.2 = (f32[2,32,1024]{2,1,0:T(8,128)S(1)}, f32[2,32,1024]{2,1,0:T(8,128)S(1)}, u32[]{:S(2)}, u32[]{:S(2)}) collective-permute-start(f32[2,32,1024]{2,1,0:T(8,128)S(1)} %get-tuple-element.56.up), channel_id=1, source_target_pairs={{0,8},{8,16},{16,24},{24,0},{1,9},{9,17},{17,25},{25,1},{2,10},{10... | collective-permute-start | bytes 786440 | tf_op jit(solution)/shard_map/ppermute | solution.py:617
  12.0 18.1 %collective-permute-start.3 = (f32[2,32,1024]{2,1,0:T(8,128)S(1)}, f32[2,32,1024]{2,1,0:T(8,128)S(1)}, u32[]{:S(2)}, u32[]{:S(2)}) collective-permute-start(f32[2,32,1024]{2,1,0:T(8,128)S(1)} %get-tuple-element.57.down), channel_id=1, source_target_pairs={{0,24},{8,0},{16,8},{24,16},{1,25},{9,1},{17,9},{25,17},{2,26},{10... | collective-permute-start | bytes 786440 | tf_op jit(solution)/shard_map/ppermute | solution.py:617
  13.1 17.9 %collective-permute-start.4 = (f32[2,16,768]{2,1,0:T(8,128)S(1)}, f32[2,16,768]{2,1,0:T(8,128)S(1)}, u32[]{:S(2)}, u32[]{:S(2)}) collective-permute-start(f32[2,16,768]{2,1,0:T(8,128)S(1)} %get-tuple-element.68), channel_id=1, source_target_pairs={{0,8},{8,16},{16,24},{24,0},{1,9},{9,17},{17,25},{25,1},{2,10},{10... | collective-permute-start | bytes 294920 | tf_op jit(solution)/shard_map/ppermute | solution.py:617
  14.1 16.8 %collective-permute-start.5 = (f32[2,16,768]{2,1,0:T(8,128)S(1)}, f32[2,16,768]{2,1,0:T(8,128)S(1)}, u32[]{:S(2)}, u32[]{:S(2)}) collective-permute-start(f32[2,16,768]{2,1,0:T(8,128)S(1)} %get-tuple-element.69), channel_id=1, source_target_pairs={{0,24},{8,0},{16,8},{24,16},{1,25},{9,1},{17,9},{25,17},{2,26},{10... | collective-permute-start | bytes 294920 | tf_op jit(solution)/shard_map/ppermute | solution.py:617
  16.7 14.3 %collective-permute-start.6 = (f32[2,16,768]{2,1,0:T(8,128)S(1)}, f32[2,16,768]{2,1,0:T(8,128)S(1)}, u32[]{:S(2)}, u32[]{:S(2)}) collective-permute-start(f32[2,16,768]{2,1,0:T(8,128)S(1)} %get-tuple-element.72), channel_id=1, source_target_pairs={{0,8},{8,16},{16,24},{24,0},{1,9},{9,17},{17,25},{25,1},{2,10},{10... | collective-permute-start | bytes 294920 | tf_op jit(solution)/shard_map/ppermute | solution.py:617
  20.2 11.9 %collective-permute-start.7 = (f32[2,16,768]{2,1,0:T(8,128)S(1)}, f32[2,16,768]{2,1,0:T(8,128)S(1)}, u32[]{:S(2)}, u32[]{:S(2)}) collective-permute-start(f32[2,16,768]{2,1,0:T(8,128)S(1)} %get-tuple-element.73), channel_id=1, source_target_pairs={{0,24},{8,0},{16,8},{24,16},{1,25},{9,1},{17,9},{25,17},{2,26},{10... | collective-permute-start | bytes 294920 | tf_op jit(solution)/shard_map/ppermute | solution.py:617
  32.2 11.0 %collective-permute-start.10 = (f32[3,32,256]{2,1,0:T(8,128)S(1)}, f32[3,32,256]{2,1,0:T(8,128)S(1)}, u32[]{:S(2)}, u32[]{:S(2)}) collective-permute-start(f32[3,32,256]{2,1,0:T(8,128)S(1)} %get-tuple-element.84), channel_id=1, source_target_pairs={{0,8},{8,0},{16,24},{24,16},{1,9},{9,1},{17,25},{25,17},{2,10},{10... | collective-permute-start | bytes 294920 | tf_op jit(solution)/shard_map/ppermute | solution.py:745
  33.8 9.5 %collective-permute-start.11 = (f32[3,32,256]{2,1,0:T(8,128)S(1)}, f32[3,32,256]{2,1,0:T(8,128)S(1)}, u32[]{:S(2)}, u32[]{:S(2)}) collective-permute-start(f32[3,32,256]{2,1,0:T(8,128)S(1)} %get-tuple-element.85), channel_id=1, source_target_pairs={{0,16},{8,24},{16,0},{24,8},{1,17},{9,25},{17,1},{25,9},{2,18},{10... | collective-permute-start | bytes 294920 | tf_op jit(solution)/shard_map/ppermute | solution.py:745
  34.3 9.0 %collective-permute-start.12 = (f32[3,32,256]{2,1,0:T(8,128)S(1)}, f32[3,32,256]{2,1,0:T(8,128)S(1)}, u32[]{:S(2)}, u32[]{:S(2)}) collective-permute-start(f32[3,32,256]{2,1,0:T(8,128)S(1)} %get-tuple-element.86), channel_id=1, source_target_pairs={{0,24},{8,16},{16,8},{24,0},{1,25},{9,17},{17,9},{25,1},{2,26},{10... | collective-permute-start | bytes 294920 | tf_op jit(solution)/shard_map/ppermute | solution.py:745
  35.8 5.2 %collective-permute-start.8 = (f32[2,32,256]{2,1,0:T(8,128)S(1)}, f32[2,32,256]{2,1,0:T(8,128)S(1)}, u32[]{:S(2)}, u32[]{:S(2)}) collective-permute-start(f32[2,32,256]{2,1,0:T(8,128)S(1)} %get-tuple-element.76), channel_id=1, source_target_pairs={{0,8},{8,16},{16,24},{24,0},{1,9},{9,17},{17,25},{25,1},{2,10},{10... | collective-permute-start | bytes 196616 | tf_op jit(solution)/shard_map/ppermute | solution.py:617
  37.3 4.3 %collective-permute-start.9 = (f32[2,32,256]{2,1,0:T(8,128)S(1)}, f32[2,32,256]{2,1,0:T(8,128)S(1)}, u32[]{:S(2)}, u32[]{:S(2)}) collective-permute-start(f32[2,32,256]{2,1,0:T(8,128)S(1)} %get-tuple-element.77), channel_id=1, source_target_pairs={{0,24},{8,0},{16,8},{24,16},{1,25},{9,1},{17,9},{25,17},{2,26},{10... | collective-permute-start | bytes 196616 | tf_op jit(solution)/shard_map/ppermute | solution.py:617
